TPU v7x, 32 devices: a whole 2x2x4 slice. The times are simulated.
32 devices in a mesh: ov: 16 (over z, y, core), vec: 2 (over x).
Axes of the slice: x: 2, y: 2, z: 4, core: 2. Of those that a mesh axis runs over, the one named last changes fastest.
Arguments:
- chol_vectors: bfloat16 [196608, 4096], P('ov', 'vec'), may hold values from -3.5 to 3.5
- amplitudes: bfloat16 [196608, 256], P('ov'), may hold values from -0.013671875 to 0.013671875
- sigma_prior: bfloat16 [196608, 256], P(('ov', 'vec')), may hold values from -4 to 4
Outputs:
- sigma_cycle: bfloat16 [196608, 256], P(('ov', 'vec'))
All inputs are finite; a program needn't handle non-finite values.
Results may differ from a plain program's by a relative error of at most 0.0065.
Values may be sent and summed in bfloat16 or wider, within the bound.
A program may use at most 128 MiB of HBM per device.

v0:
```python
import jax
import jax.numpy as jnp
from jax import lax
from jax.sharding import PartitionSpec as P


def body(chol_vectors, amplitudes, sigma_prior):
    contract = (((0,), (0,)), ((), ()))
    partial_x = lax.dot_general(
        chol_vectors, amplitudes, contract, preferred_element_type=jnp.float32
    )
    summed = lax.psum(partial_x, "ov")
    coupling = summed.astype(jnp.bfloat16)
    cycle = lax.psum_scatter(
        jnp.dot(chol_vectors, coupling, preferred_element_type=jnp.float32),
        "vec",
        scatter_dimension=0,
        tiled=True,
    )
    return (sigma_prior.astype(jnp.float32) + cycle).astype(jnp.bfloat16)


def solution(mesh):
    return jax.shard_map(
        body,
        mesh=mesh,
        in_specs=(P("ov", "vec"), P("ov", None), P(("ov", "vec"), None)),
        out_specs=P(("ov", "vec"), None),
        check_vma=False,
    )
```

profile of v0, /device:TPU:0, one launch (start us, length us, event | category | flops | bytes accessed | tf_op | source)
XLA Modules:
  0.0 287.8 jit_solution(18080904443797007626)
XLA Ops:
  6.5 0.0 reduce-scatter.2.cloned.1.call-start
  6.5 21.7 %fusion.1 = f32[2048,256]{1,0:T(8,128)S(1)} fusion(bf16[12288,2048]{1,0:T(8,128)(2,1)} %param.3, bf16[12288,256]{1,0:T(8,128)(2,1)} %param.4), kind=kOutput, calls=%fused_computation.3 | convolution fusion | flops 12884901888 | bytes 58720256 | tf_op jit(solution)/shard_map/dot_general | solution.py:9
  28.3 76.9 %all-reduce.1 = bf16[2048,256]{1,0:T(8,128)(2,1)S(1)} all-reduce(f32[2048,256]{1,0:T(8,128)S(1)} %fusion.1), channel_id=1, replica_groups=mesh['ov'=16,'vec'=2] {'ov'}, use_global_device_ids=true, to_apply=%region_0.0 | all-reduce | flops 524288 | bytes 3145728 | tf_op jit(solution)/shard_map/psum | solution.py:12
  105.1 23.9 %convolution_bitcast_fusion = f32[12288,256]{0,1:T(8,128)} fusion(bf16[12288,2048]{1,0:T(8,128)(2,1)} %param.3, bf16[2048,256]{1,0:T(8,128)(2,1)S(1)} %all-reduce.1), kind=kOutput, calls=%fused_computation | convolution fusion | flops 12884901888 | bytes 63963136 | tf_op jit(solution)/shard_map/dot_general | solution.py:15
  129.1 0.0 reduce-scatter.2.cloned.1.call-update
  129.1 3.2 %copy.4 = bf16[6144,256]{0,1:T(8,128)(2,1)S(1)} copy(bf16[6144,256]{1,0:T(8,128)(2,1)} %param.5) | data formatting | bytes 6291456 | tf_op args[2]
  132.3 138.7 %reduce-scatter.2.cloned.1.call-done = f32[6144,256]{0,1:T(8,128)} async-done(((f32[12288,256]{0,1:T(8,128)}), f32[6144,256]{0,1:T(8,128)}) %reduce-scatter.2.cloned.1.call-update) | async-done | bytes 6291472 | tf_op jit(solution)/shard_map/reduce_scatter | solution.py:14
  271.0 5.3 %add_convert_fusion = bf16[6144,256]{0,1:T(8,128)(2,1)} fusion(f32[6144,256]{0,1:T(8,128)} %reduce-scatter.2.cloned.1.call-done, bf16[6144,256]{0,1:T(8,128)(2,1)S(1)} %copy.4), kind=kLoop, calls=%fused_computation.1 | loop fusion | flops 4718592 | bytes 12582912 | tf_op jit(solution)/shard_map/convert_element_type | solution.py:20
  276.3 4.6 %copy.5 = bf16[6144,256]{1,0:T(8,128)(2,1)} copy(bf16[6144,256]{0,1:T(8,128)(2,1)} %add_convert_fusion) | data formatting | bytes 6291456 | tf_op jit(solution)/shard_map/convert_element_type | solution.py:20
Async XLA Ops:
  6.5 264.5 %reduce-scatter.2.cloned.1.call-start = ((), (), s32[]{:S(2)}) async-start(), calls=%async_computation.1 | async-start | bytes 18874368 | tf_op jit(solution)/shard_map/reduce_scatter | solution.py:14
Sparse Core Ops, SparseCore 0:
  129.2 141.7 reduce-scatter.1
where the time goes:
time: 288 us
  waiting for transfers between devices  139 us (48%)
  blocking collectives  76.9 us (27%)
  matrix products  45.6 us (16%)
  between operations  13.4 us (5%)
  local copies, waits for them, and re-layouts  7.82 us (3%)
  other arithmetic  5.28 us (2%)
    reduce_scatter x1, waiting for transfers between devices, body(): lax.psum_scatter(jnp.dot(chol_vectors, coupling, preferred_element_type=j...  139 us
    psum x1, blocking collectives, body(): summed = lax.psum(partial_x, 'ov')  76.9 us
    dot_general x1, matrix products, body(): jnp.dot(chol_vectors, coupling, preferred_element_type=jnp.float32)  23.9 us
    dot_general x1, matrix products, body(): lax.dot_general(chol_vectors, amplitudes, contract, preferred_element_typ...  21.7 us
  transfers between devices with their start and end apart: 1, of which 1 were waited for; matrix products, arithmetic and copies ran while one was open for 1% of the time, Pallas kernels for 0%

commit v1 on v0

--- a/solution.py
+++ b/solution.py
@@ -9,7 +9,9 @@
     partial_x = lax.dot_general(
         chol_vectors, amplitudes, contract, preferred_element_type=jnp.float32
     )
-    summed = lax.psum(partial_x, "ov")
+    summed = partial_x
+    for hop in (1, 2, 4, 8):
+        summed = summed + lax.ppermute(summed, "ov", [(dev, dev ^ hop) for dev in range(16)])
     coupling = summed.astype(jnp.bfloat16)
     cycle = lax.psum_scatter(
         jnp.dot(chol_vectors, coupling, preferred_element_type=jnp.float32),

time: 288 us -> 409 us (1.42)
  waiting for transfers between devices: 139 us -> 327 us
  blocking collectives: 76.9 us -> 0 us
  starting transfers between devices: 0.01 us -> 7.96 us
    ppermute x0 -> x4, waiting for transfers between devices: none -> 185 us  [body(): lax.ppermute(summed, 'ov', [(dev, dev ^ hop) for dev in range(16)])]
    psum x1 -> x0, blocking collectives: 76.9 us -> none  [body(): summed = lax.psum(partial_x, 'ov')]
    ppermute x0 -> x4, starting transfers between devices: none -> 7.96 us  [body(): lax.ppermute(summed, 'ov', [(dev, dev ^ hop) for dev in range(16)])]
  transfers between devices with their start and end apart: 1 -> 5, of which waited for: 1 -> 5; matrix products, arithmetic and copies ran while one was open for 1% -> 1% of each run, Pallas kernels for 0% -> 0%
where the time goes in v1:
time: 409 us; the launch traced here: 408 us
  waiting for transfers between devices  327 us (80%)
  matrix products  46.2 us (11%)
  between operations  13.4 us (3%)
  starting transfers between devices  7.96 us (2%)
  local copies, waits for them, and re-layouts  7.82 us (2%)
  other arithmetic  6.07 us (1%)
    ppermute x4, waiting for transfers between devices, body(): lax.ppermute(summed, 'ov', [(dev, dev ^ hop) for dev in range(16)])  185 us
    reduce_scatter x1, waiting for transfers between devices, body(): lax.psum_scatter(jnp.dot(chol_vectors, coupling, preferred_element_type=j...  142 us
    dot_general x1, matrix products, body(): jnp.dot(chol_vectors, coupling, preferred_element_type=jnp.float32)  24.5 us
    dot_general x1, matrix products, body(): lax.dot_general(chol_vectors, amplitudes, contract, preferred_element_typ...  21.7 us
  transfers between devices with their start and end apart: 5, of which 5 were waited for; matrix products, arithmetic and copies ran while one was open for 1% of the time, Pallas kernels for 0%

profile of v1, /device:TPU:0, one launch (start us, length us, event | category | flops | bytes accessed | tf_op | source)
XLA Modules:
  0.0 408.4 jit_solution(15865993328646608873)
XLA Ops:
  6.5 0.0 reduce-scatter.2.cloned.1.call-start
  6.5 21.7 %fusion = f32[2048,256]{1,0:T(8,128)S(1)} fusion(bf16[12288,2048]{1,0:T(8,128)(2,1)} %param.3, bf16[12288,256]{1,0:T(8,128)(2,1)} %param.4), kind=kOutput, calls=%fused_computation.3 | convolution fusion | flops 12884901888 | bytes 58720256 | tf_op jit(solution)/shard_map/dot_general | solution.py:9
  28.3 0.6 collective-permute-start
  28.8 3.8 collective-permute-done
  32.6 0.3 add.17
  32.9 2.9 collective-permute-start.1
  35.8 45.9 %collective-permute-done.1 = f32[2048,256]{1,0:T(8,128)S(1)} collective-permute-done((f32[2048,256]{1,0:T(8,128)S(1)}, f32[2048,256]{1,0:T(8,128)S(1)}, u32[]{:S(2)}, u32[]{:S(2)}) %collective-permute-start.1) | collective-permute-done | bytes 2097184 | tf_op jit(solution)/shard_map/ppermute | solution.py:14
  81.7 0.3 add.18
  82.0 1.9 collective-permute-start.2
  83.9 45.3 %collective-permute-done.2 = f32[2048,256]{1,0:T(8,128)S(1)} collective-permute-done((f32[2048,256]{1,0:T(8,128)S(1)}, f32[2048,256]{1,0:T(8,128)S(1)}, u32[]{:S(2)}, u32[]{:S(2)}) %collective-permute-start.2) | collective-permute-done | bytes 2097184 | tf_op jit(solution)/shard_map/ppermute | solution.py:14
  129.2 0.3 add.19
  129.4 2.6 collective-permute-start.3
  132.0 89.7 %collective-permute-done.3 = f32[2048,256]{1,0:T(8,128)} collective-permute-done((f32[2048,256]{1,0:T(8,128)S(1)}, f32[2048,256]{1,0:T(8,128)}, u32[]{:S(2)}, u32[]{:S(2)}) %collective-permute-start.3) | collective-permute-done | bytes 2097184 | tf_op jit(solution)/shard_map/ppermute | solution.py:14
  221.7 24.5 %convolution_bitcast_fusion = f32[12288,256]{0,1:T(8,128)} fusion(bf16[12288,2048]{1,0:T(8,128)(2,1)} %param.3, f32[2048,256]{1,0:T(8,128)S(1)} %add.19, f32[2048,256]{1,0:T(8,128)} %collective-permute-done.3), kind=kOutput, calls=%fused_computation | convolution fusion | flops 12885950464 | bytes 67108864 | tf_op jit(solution)/shard_map/dot_general | solution.py:17
  246.2 0.0 reduce-scatter.2.cloned.1.call-update
  246.2 3.2 copy.4
  249.4 142.3 %reduce-scatter.2.cloned.1.call-done = f32[6144,256]{0,1:T(8,128)} async-done(((f32[12288,256]{0,1:T(8,128)}), f32[6144,256]{0,1:T(8,128)}) %reduce-scatter.2.cloned.1.call-update) | async-done | bytes 6291472 | tf_op jit(solution)/shard_map/reduce_scatter | solution.py:16
  391.7 5.3 %add_convert_fusion = bf16[6144,256]{0,1:T(8,128)(2,1)} fusion(f32[6144,256]{0,1:T(8,128)} %reduce-scatter.2.cloned.1.call-done, bf16[6144,256]{0,1:T(8,128)(2,1)S(1)} %copy.4), kind=kLoop, calls=%fused_computation.1 | loop fusion | flops 4718592 | bytes 12582912 | tf_op jit(solution)/shard_map/convert_element_type | solution.py:22
  397.0 4.6 %copy.5 = bf16[6144,256]{1,0:T(8,128)(2,1)} copy(bf16[6144,256]{0,1:T(8,128)(2,1)} %add_convert_fusion) | data formatting | bytes 6291456 | tf_op jit(solution)/shard_map/convert_element_type | solution.py:22
Async XLA Ops:
  6.5 385.2 %reduce-scatter.2.cloned.1.call-start = ((), (), s32[]{:S(2)}) async-start(), calls=%async_computation.1 | async-start | bytes 18874368 | tf_op jit(solution)/shard_map/reduce_scatter | solution.py:16
  28.3 4.3 %collective-permute-start = (f32[2048,256]{1,0:T(8,128)S(1)}, f32[2048,256]{1,0:T(8,128)S(1)}, u32[]{:S(2)}, u32[]{:S(2)}) collective-permute-start(f32[2048,256]{1,0:T(8,128)S(1)} %fusion), channel_id=1, source_target_pairs={{0,2},{2,0},{4,6},{6,4},{8,10},{10,8},{12,14},{14,12},{16,18},{18,... | collective-permute-start | bytes 6291464 | tf_op jit(solution)/shard_map/ppermute | solution.py:14
  32.9 48.9 %collective-permute-start.1 = (f32[2048,256]{1,0:T(8,128)S(1)}, f32[2048,256]{1,0:T(8,128)S(1)}, u32[]{:S(2)}, u32[]{:S(2)}) collective-permute-start(f32[2048,256]{1,0:T(8,128)S(1)} %add.17), channel_id=1, source_target_pairs={{0,4},{2,6},{4,0},{6,2},{8,12},{10,14},{12,8},{14,10},{16,20},{18,... | collective-permute-start | bytes 6291464 | tf_op jit(solution)/shard_map/ppermute | solution.py:14
  82.0 47.2 %collective-permute-start.2 = (f32[2048,256]{1,0:T(8,128)S(1)}, f32[2048,256]{1,0:T(8,128)S(1)}, u32[]{:S(2)}, u32[]{:S(2)}) collective-permute-start(f32[2048,256]{1,0:T(8,128)S(1)} %add.18), channel_id=1, source_target_pairs={{0,8},{2,10},{4,12},{6,14},{8,0},{10,2},{12,4},{14,6},{16,24},{18,... | collective-permute-start | bytes 6291464 | tf_op jit(solution)/shard_map/ppermute | solution.py:14
  129.4 92.3 %collective-permute-start.3 = (f32[2048,256]{1,0:T(8,128)S(1)}, f32[2048,256]{1,0:T(8,128)}, u32[]{:S(2)}, u32[]{:S(2)}) collective-permute-start(f32[2048,256]{1,0:T(8,128)S(1)} %add.19), channel_id=1, source_target_pairs={{0,16},{2,18},{4,20},{6,22},{8,24},{10,26},{12,28},{14,30},{16,0},... | collective-permute-start | bytes 6291464 | tf_op jit(solution)/shard_map/ppermute | solution.py:14
Sparse Core Ops, SparseCore 0:
  246.3 145.3 reduce-scatter.1
